TPU v7x, 32 devices: a whole 2x2x4 slice. The times are simulated.
32 devices in a mesh: fft: 16 (over z, x, core), scal: 2 (over y).
Axes of the slice: x: 2, y: 2, z: 4, core: 2. Of those that a mesh axis runs over, the one named last changes fastest.
Arguments:
- scalar_state: float32 [2, 2, 256, 256, 128], P('scal', None, 'fft'), may hold values from -12 to 12
- velocity: bfloat16 [3, 256, 256, 256], P(None, 'fft', 'scal'), may hold values from -6 to 6
- species: int32 [2], P('scal'), may hold values from 0 to 63
- kappa_table: float32 [64], replicated, may hold values from 0.1 to 1
- dealias_bound: int32 [2], P('scal'), may hold values from 64 to 85
Outputs:
- new_state: float32 [2, 2, 256, 256, 128], P('scal', None, 'fft')
- kappa: float32 [2], P('scal')
All inputs are finite; a program needn't handle non-finite values.
Results may differ from a plain program's by a relative error of at most 0.0027.
Values may be sent and summed in bfloat16 or wider, within the bound.
A program may use at most 128 MiB of HBM per device.

v0:
```python
import math

import jax
import jax.numpy as jnp
from jax import lax
from jax.sharding import PartitionSpec as P

cfl_number = 0.2


def twiddle(size_in, size_out, length):
    row_index = jnp.arange(size_in, dtype=jnp.int32)[:, None]
    col_index = jnp.arange(size_out, dtype=jnp.int32)[None, :]
    angles = (row_index * col_index % length).astype(jnp.float32) * (2.0 * math.pi / length)
    norming = 1.0 / math.sqrt(length)
    return (jnp.cos(angles) * norming, jnp.sin(angles) * norming)


def build_tables(length):
    half_len = length // 2
    full_cos, full_sin = twiddle(length, length, length)
    inv_cos, inv_sin = twiddle(half_len, length, length)
    weight = jnp.where(jnp.arange(half_len, dtype=jnp.int32) == 0, 1.0, 2.0).astype(jnp.float32)[
        :, None
    ]
    fwd_cos, fwd_sin = twiddle(length, half_len, length)
    listed = (full_cos, full_sin, inv_cos * weight, inv_sin * weight, fwd_cos, fwd_sin)
    return tuple((matrix.astype(jnp.bfloat16) for matrix in listed))


def product(formula, operand, matrix):
    return jnp.einsum(formula, operand, matrix, preferred_element_type=jnp.float32)


def complex_section(real_part, imag_part, cos_matrix, sin_matrix, formula, inverse):
    real_cos = product(formula, real_part, cos_matrix)
    real_sin = product(formula, real_part, sin_matrix)
    imag_cos = product(formula, imag_part, cos_matrix)
    imag_sin = product(formula, imag_part, sin_matrix)
    if inverse:
        return (real_cos - imag_sin, real_sin + imag_cos)
    return (real_cos + imag_sin, imag_cos - real_sin)


def times_wave(wavenumber, real_part, imag_part):
    new_real = (-wavenumber * imag_part.astype(jnp.float32)).astype(jnp.bfloat16)
    new_imag = (wavenumber * real_part.astype(jnp.float32)).astype(jnp.bfloat16)
    return (new_real, new_imag)


def body(scalar_state, velocity, species, kappa_table, dealias_bound):
    ky_local = scalar_state.shape[2]
    length = scalar_state.shape[3]
    half_len = length // 2
    total_count = kappa_table.shape[0]
    full_cos, full_sin, inv_cos, inv_sin, fwd_cos, fwd_sin = build_tables(length)
    ky_index = lax.axis_index("fft") * ky_local + jnp.arange(ky_local, dtype=jnp.int32)
    ky_wave = jnp.where(ky_index < half_len, ky_index, ky_index - length).astype(jnp.float32)[
        :, None, None
    ]
    kz_index = jnp.arange(length, dtype=jnp.int32)
    signed_full = jnp.where(kz_index < half_len, kz_index, kz_index - length).astype(jnp.float32)
    kz_wave = signed_full[None, :, None]
    ky_whole = signed_full[:, None, None]
    kx_wave = jnp.arange(half_len, dtype=jnp.int32).astype(jnp.float32)[None, None, :]
    ksquare = kx_wave * kx_wave + ky_wave * ky_wave + kz_wave * kz_wave
    weight = jnp.where(kx_wave == 0.0, 1.0, 2.0).astype(jnp.float32)
    cell_count = float(length) ** 3
    step_size = cfl_number * 2.0 * math.pi / length
    speeds = lax.all_gather(velocity, "scal", axis=2, tiled=True)

    def finish_inverse(halves):
        y_section = complex_section(
            halves[0], halves[1], full_cos, full_sin, "...yzx,yw->...zwx", True
        )
        y_real = y_section[0].astype(jnp.bfloat16)
        y_imag = y_section[1].astype(jnp.bfloat16)
        return product("...zwk,kx->...zwx", y_real, inv_cos) - product(
            "...zwk,kx->...zwx", y_imag, inv_sin
        )

    def gradient_set(real_part, imag_part):
        pair_real = jnp.stack([real_part, -kz_wave * imag_part]).astype(jnp.bfloat16)
        pair_imag = jnp.stack([imag_part, kz_wave * real_part]).astype(jnp.bfloat16)
        z_section = complex_section(
            pair_real, pair_imag, full_cos, full_sin, "...ykx,kz->...yzx", True
        )
        z_real = z_section[0].astype(jnp.bfloat16)
        z_imag = z_section[1].astype(jnp.bfloat16)
        came_real, came_imag = (
            lax.all_to_all(z_real, "fft", split_axis=2, concat_axis=1, tiled=True),
            lax.all_to_all(z_imag, "fft", split_axis=2, concat_axis=1, tiled=True),
        )
        x_real, x_imag = times_wave(kx_wave, came_real[0], came_imag[0])
        y_real, y_imag = times_wave(ky_whole, came_real[0], came_imag[0])
        all_real = jnp.stack([x_real, y_real, came_real[1]])
        all_imag = jnp.stack([x_imag, y_imag, came_imag[1]])
        return finish_inverse((all_real, all_imag))

    def advect(gradients):
        total = speeds[0].astype(jnp.float32) * gradients[0]
        total = total + speeds[1].astype(jnp.float32) * gradients[1]
        total = total + speeds[2].astype(jnp.float32) * gradients[2]
        return total.astype(jnp.bfloat16)

    def finish_forward(halves):
        return complex_section(halves[0], halves[1], full_cos, full_sin, "...wzk,zv->...wvk", False)

    def tendency(advected, bound):
        real_x = product("zyx,xk->zyk", advected, fwd_cos).astype(jnp.bfloat16)
        imag_x = (-product("zyx,xk->zyk", advected, fwd_sin)).astype(jnp.bfloat16)
        y_section = complex_section(real_x, imag_x, full_cos, full_sin, "zyk,yw->wzk", False)
        y_real = y_section[0].astype(jnp.bfloat16)
        y_imag = y_section[1].astype(jnp.bfloat16)
        spectral = finish_forward(
            (
                lax.all_to_all(y_real, "fft", split_axis=0, concat_axis=1, tiled=True),
                lax.all_to_all(y_imag, "fft", split_axis=0, concat_axis=1, tiled=True),
            )
        )
        dealias_mask = (ksquare <= bound * bound).astype(jnp.float32)
        return (-dealias_mask * spectral[0], -dealias_mask * spectral[1])

    scalar = 0
    start_real = scalar_state[scalar, 0]
    start_imag = scalar_state[scalar, 1]
    energy = start_real * start_real + start_imag * start_imag
    local_var = [jnp.sum(weight * energy) / cell_count]
    local_grad = [jnp.sum(weight * ksquare * energy) / cell_count]
    gradients = gradient_set(start_real, start_imag)
    magnitude = jnp.sqrt(
        gradients[0] * gradients[0] + gradients[1] * gradients[1] + gradients[2] * gradients[2]
    )
    local_peak = [jnp.max(magnitude)]
    advect_saved = [advect(gradients)]
    var_part = jnp.stack(local_var)
    grad_part = jnp.stack(local_grad)
    peak_part = jnp.stack(local_peak)
    variance, mean_grad = lax.psum((var_part, grad_part), "fft")
    peak_value = lax.pmax(peak_part, "fft")
    matches = species[:, None] == jnp.arange(total_count, dtype=jnp.int32)[None, :]
    base_kappa = jnp.sum(jnp.where(matches, kappa_table[None, :], 0.0), axis=1)
    kappa = base_kappa * peak_value * jnp.sqrt(variance) / (mean_grad + 1e-06)
    scalar = 0
    start_real = scalar_state[scalar, 0]
    start_imag = scalar_state[scalar, 1]
    factor = jnp.exp(-kappa[scalar] * ksquare * step_size)
    bound = dealias_bound[scalar].astype(jnp.float32)
    first_real, first_imag = tendency(advect_saved[scalar], bound)
    mid_real = factor * (start_real + step_size * first_real)
    mid_imag = factor * (start_imag + step_size * first_imag)
    second_real, second_imag = tendency(advect(gradient_set(mid_real, mid_imag)), bound)
    new_real = factor * start_real + 0.5 * step_size * (factor * first_real + second_real)
    new_imag = factor * start_imag + 0.5 * step_size * (factor * first_imag + second_imag)
    updated_list = [jnp.stack([new_real, new_imag])]
    return (jnp.stack(updated_list), kappa)


def solution(mesh):
    placed = (
        P("scal", None, "fft", None, None),
        P(None, "fft", "scal", None),
        P("scal"),
        P(),
        P("scal"),
    )
    return jax.shard_map(
        body,
        mesh=mesh,
        in_specs=placed,
        out_specs=(P("scal", None, "fft", None, None), P("scal")),
        check_vma=False,
    )
```

profile of v0, /device:TPU:0, one launch (start us, length us, event | category | flops | bytes accessed | tf_op | source)
XLA Modules:
  0.0 544.3 jit_solution(1776327295158472400)
XLA Ops:
  17.1 7.4 %all-to-all-start.1 = ((bf16[2,16,256,128]{3,1,0,2:T(8,128)(2,1)}), bf16[2,16,256,128]{3,1,0,2:T(8,128)(2,1)}, u32[]{:S(2)}, u32[]{:S(2)}) async-start(bf16[2,16,256,128]{3,1,0,2:T(8,128)(2,1)} %copy.48), calls=%async_computation.1 | async-start | bytes 4194304 | tf_op jit(solution)/shard_map/all_to_all | solution.py:91
  30.5 35.1 %all-to-all-done.1 = bf16[2,16,256,128]{3,1,0,2:T(8,128)(2,1)} async-done(((bf16[2,16,256,128]{3,1,0,2:T(8,128)(2,1)}), bf16[2,16,256,128]{3,1,0,2:T(8,128)(2,1)}, u32[]{:S(2)}, u32[]{:S(2)}) %all-to-all-start.1) | async-done | bytes 2097184 | tf_op jit(solution)/shard_map/all_to_all | solution.py:91
  65.6 11.2 %all-to-all-start = ((bf16[2,16,256,128]{3,1,0,2:T(8,128)(2,1)}), bf16[2,16,256,128]{3,1,0,2:T(8,128)(2,1)S(1)}, u32[]{:S(2)}, u32[]{:S(2)}) async-start(bf16[2,16,256,128]{3,1,0,2:T(8,128)(2,1)} %copy.43), calls=%async_computation | async-start | bytes 4194304 | tf_op jit(solution)/shard_map/all_to_all | solution.py:92
  83.2 34.6 %all-to-all-done = bf16[2,16,256,128]{3,1,0,2:T(8,128)(2,1)S(1)} async-done(((bf16[2,16,256,128]{3,1,0,2:T(8,128)(2,1)}), bf16[2,16,256,128]{3,1,0,2:T(8,128)(2,1)S(1)}, u32[]{:S(2)}, u32[]{:S(2)}) %all-to-all-start) | async-done | bytes 2097184 | tf_op jit(solution)/shard_map/all_to_all | solution.py:92
  132.2 11.1 %fusion.7 = f32[3,16,256,256]{3,2,1,0:T(8,128)} fusion(f32[256,3,16,128]{3,0,2,1:T(8,128)} %fusion.58, bf16[1,256,16,128]{3,1,2,0:T(8,128)(2,1)S(1)} %copy.56, bf16[1,256,16,128]{3,1,2,0:T(8,128)(2,1)S(1)} %get-tuple-element.27, bf16[1,256,16,128]{3,1,2,0:T(8,128)(2,1)S(1)} %get-tuple-element.26, f32[128]{0:T(128)S(1)} %fusion.137), kind=kOutput, calls=%fused_computation.28 | convolution fusion | flops 1624768512 | bytes 22020608 | tf_op jit(solution)/shard_map/...zwk,kx->...zwx/dot_general | solution.py:32
  143.2 11.4 %convolution_subtract_fusion.1 = f32[3,16,256,256]{3,2,1,0:T(8,128)} fusion(f32[3,16,256,256]{3,2,1,0:T(8,128)} %fusion.7, f32[256,3,16,128]{3,0,2,1:T(8,128)} %fusion.57, bf16[1,256,16,128]{3,1,2,0:T(8,128)(2,1)S(1)} %copy.56, bf16[1,256,16,128]{3,1,2,0:T(8,128)(2,1)S(1)} %get-tuple-element.27, bf16[1,256,16,128]{3,1,2,0:T(8,128)(2,1)S(1)} %get-tuple-element.26, ...), kind=kOutput, calls=%fused_computation.11 | convolution fusion | flops 1627914240 | bytes 34603520 | tf_op jit(solution)/shard_map/...zwk,kx->...zwx/dot_general | solution.py:32
  154.6 6.3 %all-gather.2.cloned.1.call-done = bf16[3,16,256,256]{3,2,1,0:T(8,128)(2,1)} async-done(((bf16[3,16,128,256]{3,2,1,0:T(8,128)(2,1)}), bf16[3,16,256,256]{3,2,1,0:T(8,128)(2,1)}) %all-gather.2.cloned.1.call-update) | async-done | bytes 6291472 | tf_op jit(solution)/shard_map/all_gather | solution.py:70
  160.9 8.5 %sqrt_reduce_fusion = (f32[]{:T(128)}, bf16[16,256,256]{2,1,0:T(8,128)(2,1)S(1)}) fusion(f32[3,16,256,256]{3,2,1,0:T(8,128)} %convolution_subtract_fusion.1, bf16[3,16,256,256]{3,2,1,0:T(8,128)(2,1)} %all-gather.2.cloned.1.call-done), kind=kLoop, calls=%fused_computation.19 | loop fusion | flops 15728639 | bytes 20971524 | tf_op jit(solution)/shard_map/reduce_max | solution.py:134
  176.1 5.6 %all-to-all-start.3 = ((bf16[256,16,128]{2,1,0:T(8,128)(2,1)}), bf16[256,16,128]{2,1,0:T(8,128)(2,1)S(1)}, u32[]{:S(2)}, u32[]{:S(2)}) async-start(bf16[256,16,128]{2,1,0:T(8,128)(2,1)} %copy.59), calls=%async_computation.3 | async-start | bytes 2097152 | tf_op jit(solution)/shard_map/all_to_all | solution.py:118
  186.0 18.5 %all-to-all-done.3 = bf16[256,16,128]{2,1,0:T(8,128)(2,1)S(1)} async-done(((bf16[256,16,128]{2,1,0:T(8,128)(2,1)}), bf16[256,16,128]{2,1,0:T(8,128)(2,1)S(1)}, u32[]{:S(2)}, u32[]{:S(2)}) %all-to-all-start.3) | async-done | bytes 1048608 | tf_op jit(solution)/shard_map/all_to_all | solution.py:118
  204.6 6.8 %all-to-all-start.2 = ((bf16[256,16,128]{2,1,0:T(8,128)(2,1)}), bf16[256,16,128]{2,1,0:T(8,128)(2,1)}, u32[]{:S(2)}, u32[]{:S(2)}) async-start(bf16[256,16,128]{2,1,0:T(8,128)(2,1)} %copy.57), calls=%async_computation.2 | async-start | bytes 2097152 | tf_op jit(solution)/shard_map/all_to_all | solution.py:117
  216.4 40.9 %all-reduce = (f32[1]{0:T(128)}, f32[1]{0:T(128)}) all-reduce(f32[1]{0:T(128)} %bitcast.31, f32[1]{0:T(128)} %bitcast.32), channel_id=1, replica_groups=mesh['fft'=16,'scal'=2] {'fft'}, use_global_device_ids=true, to_apply=%region_4.5 | all-reduce | flops 2 | bytes 16 | tf_op jit(solution)/shard_map/psum | solution.py:139
  260.7 30.1 %pmax.7 = f32[1]{0:T(128)} all-reduce(f32[1]{0:T(128)} %bitcast.28), channel_id=1, replica_groups=mesh['fft'=16,'scal'=2] {'fft'}, use_global_device_ids=true, to_apply=%region_2.3 | all-reduce | flops 1 | bytes 8 | tf_op jit(solution)/shard_map/pmax | solution.py:140
  308.3 4.6 all-to-all-start.5
  320.3 33.6 %all-to-all-done.5 = bf16[2,16,256,128]{3,1,0,2:T(8,128)(2,1)} async-done(((bf16[2,16,256,128]{3,1,0,2:T(8,128)(2,1)}), bf16[2,16,256,128]{3,1,0,2:T(8,128)(2,1)}, u32[]{:S(2)}, u32[]{:S(2)}) %all-to-all-start.5) | async-done | bytes 2097184 | tf_op jit(solution)/shard_map/all_to_all | solution.py:91
  353.8 11.2 %all-to-all-start.4 = ((bf16[2,16,256,128]{3,1,0,2:T(8,128)(2,1)}), bf16[2,16,256,128]{3,1,0,2:T(8,128)(2,1)}, u32[]{:S(2)}, u32[]{:S(2)}) async-start(bf16[2,16,256,128]{3,1,0,2:T(8,128)(2,1)} %copy.61), calls=%async_computation.4 | async-start | bytes 4194304 | tf_op jit(solution)/shard_map/all_to_all | solution.py:92
  369.7 36.4 %all-to-all-done.4 = bf16[2,16,256,128]{3,1,0,2:T(8,128)(2,1)} async-done(((bf16[2,16,256,128]{3,1,0,2:T(8,128)(2,1)}), bf16[2,16,256,128]{3,1,0,2:T(8,128)(2,1)}, u32[]{:S(2)}, u32[]{:S(2)}) %all-to-all-start.4) | async-done | bytes 2097184 | tf_op jit(solution)/shard_map/all_to_all | solution.py:92
  422.9 11.9 %fusion.12 = f32[3,16,256,256]{3,2,1,0:T(8,128)} fusion(f32[256,3,16,128]{3,0,2,1:T(8,128)} %fusion.56, bf16[1,256,16,128]{3,1,2,0:T(8,128)(2,1)} %copy.74, bf16[1,256,16,128]{3,1,2,0:T(8,128)(2,1)} %get-tuple-element.19, bf16[1,256,16,128]{3,1,2,0:T(8,128)(2,1)S(1)} %get-tuple-element.18, f32[128]{0:T(128)S(1)} %fusion.137), kind=kOutput, calls=%fused_computation.31 | convolution fusion | flops 1624768512 | bytes 22020608 | tf_op jit(solution)/shard_map/...zwk,kx->...zwx/dot_general | solution.py:32
  434.9 12.0 %convolution_subtract_fusion = f32[3,16,256,256]{3,2,1,0:T(8,128)} fusion(f32[3,16,256,256]{3,2,1,0:T(8,128)} %fusion.12, f32[256,3,16,128]{3,0,2,1:T(8,128)} %fusion.55, bf16[1,256,16,128]{3,1,2,0:T(8,128)(2,1)} %copy.74, bf16[1,256,16,128]{3,1,2,0:T(8,128)(2,1)} %get-tuple-element.19, bf16[1,256,16,128]{3,1,2,0:T(8,128)(2,1)S(1)} %get-tuple-element.18, ...), kind=kOutput, calls=%fused_computation.10 | convolution fusion | flops 1627914240 | bytes 34603520 | tf_op jit(solution)/shard_map/...zwk,kx->...zwx/dot_general | solution.py:32
  446.9 7.2 %fusion.42 = bf16[16,256,256]{2,1,0:T(8,128)(2,1)S(1)} fusion(f32[3,16,256,256]{3,2,1,0:T(8,128)} %convolution_subtract_fusion, bf16[3,16,256,256]{3,2,1,0:T(8,128)(2,1)} %all-gather.2.cloned.1.call-done), kind=kLoop, calls=%fused_computation.59 | loop fusion | flops 9437184 | bytes 20971520 | tf_op jit(solution)/shard_map/add | solution.py:103
  460.8 11.4 %all-to-all-start.7 = ((bf16[256,16,128]{2,1,0:T(8,128)(2,1)}), bf16[256,16,128]{2,1,0:T(8,128)(2,1)}, u32[]{:S(2)}, u32[]{:S(2)}) async-start(bf16[256,16,128]{2,1,0:T(8,128)(2,1)} %copy.77), calls=%async_computation.7 | async-start | bytes 2097152 | tf_op jit(solution)/shard_map/all_to_all | solution.py:118
  476.7 18.5 %all-to-all-done.7 = bf16[256,16,128]{2,1,0:T(8,128)(2,1)} async-done(((bf16[256,16,128]{2,1,0:T(8,128)(2,1)}), bf16[256,16,128]{2,1,0:T(8,128)(2,1)}, u32[]{:S(2)}, u32[]{:S(2)}) %all-to-all-start.7) | async-done | bytes 1048608 | tf_op jit(solution)/shard_map/all_to_all | solution.py:118
  495.2 6.8 %all-to-all-start.6 = ((bf16[256,16,128]{2,1,0:T(8,128)(2,1)}), bf16[256,16,128]{2,1,0:T(8,128)(2,1)}, u32[]{:S(2)}, u32[]{:S(2)}) async-start(bf16[256,16,128]{2,1,0:T(8,128)(2,1)} %copy.75), calls=%async_computation.6 | async-start | bytes 2097152 | tf_op jit(solution)/shard_map/all_to_all | solution.py:117
  506.2 18.7 %all-to-all-done.6 = bf16[256,16,128]{2,1,0:T(8,128)(2,1)} async-done(((bf16[256,16,128]{2,1,0:T(8,128)(2,1)}), bf16[256,16,128]{2,1,0:T(8,128)(2,1)}, u32[]{:S(2)}, u32[]{:S(2)}) %all-to-all-start.6) | async-done | bytes 1048608 | tf_op jit(solution)/shard_map/all_to_all | solution.py:117
  (120 shorter events, 122.9 us)
Async XLA Ops:
  7.2 3.5 copy-start
  11.2 1.6 copy-start.9
  17.1 48.5 %all-to-all-start.1 = ((bf16[2,16,256,128]{3,1,0,2:T(8,128)(2,1)}), bf16[2,16,256,128]{3,1,0,2:T(8,128)(2,1)}, u32[]{:S(2)}, u32[]{:S(2)}) async-start(bf16[2,16,256,128]{3,1,0,2:T(8,128)(2,1)} %copy.48), calls=%async_computation.1 | async-start | bytes 4194304 | tf_op jit(solution)/shard_map/all_to_all | solution.py:91
  24.6 1.6 copy-start.10
  65.6 52.2 %all-to-all-start = ((bf16[2,16,256,128]{3,1,0,2:T(8,128)(2,1)}), bf16[2,16,256,128]{3,1,0,2:T(8,128)(2,1)S(1)}, u32[]{:S(2)}, u32[]{:S(2)}) async-start(bf16[2,16,256,128]{3,1,0,2:T(8,128)(2,1)} %copy.43), calls=%async_computation | async-start | bytes 4194304 | tf_op jit(solution)/shard_map/all_to_all | solution.py:92
  76.8 84.1 %all-gather.2.cloned.1.call-start = ((), (), s32[]{:S(2)}) async-start(), calls=%async_computation.8 | async-start | bytes 9437184 | tf_op jit(solution)/shard_map/all_gather | solution.py:70
  119.2 1.6 copy-start.12
  176.1 28.5 %all-to-all-start.3 = ((bf16[256,16,128]{2,1,0:T(8,128)(2,1)}), bf16[256,16,128]{2,1,0:T(8,128)(2,1)S(1)}, u32[]{:S(2)}, u32[]{:S(2)}) async-start(bf16[256,16,128]{2,1,0:T(8,128)(2,1)} %copy.59), calls=%async_computation.3 | async-start | bytes 2097152 | tf_op jit(solution)/shard_map/all_to_all | solution.py:118
  204.6 89.1 %all-to-all-start.2 = ((bf16[256,16,128]{2,1,0:T(8,128)(2,1)}), bf16[256,16,128]{2,1,0:T(8,128)(2,1)}, u32[]{:S(2)}, u32[]{:S(2)}) async-start(bf16[256,16,128]{2,1,0:T(8,128)(2,1)} %copy.57), calls=%async_computation.2 | async-start | bytes 2097152 | tf_op jit(solution)/shard_map/all_to_all | solution.py:117
  211.5 48.5 %copy-start.16 = (f32[64]{0:T(128)S(1)}, f32[64]{0:T(128)}, u32[]{:S(2)}) copy-start(f32[64]{0:T(128)} %param.8) | copy-start | bytes 772
  298.0 1.5 copy-start.3
  298.0 2.9 copy-start.1
  302.3 1.6 copy-start.4
  302.3 1.6 copy-start.5
  302.3 1.7 copy-start.7
  308.3 45.6 %all-to-all-start.5 = ((bf16[2,16,256,128]{3,1,0,2:T(8,128)(2,1)}), bf16[2,16,256,128]{3,1,0,2:T(8,128)(2,1)}, u32[]{:S(2)}, u32[]{:S(2)}) async-start(bf16[2,16,256,128]{3,1,0,2:T(8,128)(2,1)} %copy.66), calls=%async_computation.5 | async-start | bytes 4194304 | tf_op jit(solution)/shard_map/all_to_all | solution.py:91
  312.9 3.0 copy-start.6
  312.9 3.0 copy-start.8
  353.8 52.3 %all-to-all-start.4 = ((bf16[2,16,256,128]{3,1,0,2:T(8,128)(2,1)}), bf16[2,16,256,128]{3,1,0,2:T(8,128)(2,1)}, u32[]{:S(2)}, u32[]{:S(2)}) async-start(bf16[2,16,256,128]{3,1,0,2:T(8,128)(2,1)} %copy.61), calls=%async_computation.4 | async-start | bytes 4194304 | tf_op jit(solution)/shard_map/all_to_all | solution.py:92
  419.1 1.8 copy-start.11
  460.8 34.3 %all-to-all-start.7 = ((bf16[256,16,128]{2,1,0:T(8,128)(2,1)}), bf16[256,16,128]{2,1,0:T(8,128)(2,1)}, u32[]{:S(2)}, u32[]{:S(2)}) async-start(bf16[256,16,128]{2,1,0:T(8,128)(2,1)} %copy.77), calls=%async_computation.7 | async-start | bytes 2097152 | tf_op jit(solution)/shard_map/all_to_all | solution.py:118
  472.3 1.3 copy-start.14
  495.2 29.8 %all-to-all-start.6 = ((bf16[256,16,128]{2,1,0:T(8,128)(2,1)}), bf16[256,16,128]{2,1,0:T(8,128)(2,1)}, u32[]{:S(2)}, u32[]{:S(2)}) async-start(bf16[256,16,128]{2,1,0:T(8,128)(2,1)} %copy.75), calls=%async_computation.6 | async-start | bytes 2097152 | tf_op jit(solution)/shard_map/all_to_all | solution.py:117
  525.0 3.0 copy-start.2
  (2 other events, 2.4 us)
Sparse Core Ops, SparseCore 0:
  79.2 81.6 all-gather.1
where the time goes:
time: 554 us; the launch traced here: 544 us
  waiting for transfers between devices  202 us (36%)
  matrix products  110 us (20%)
  blocking collectives  71 us (13%)
  starting transfers between devices  65.7 us (12%)
  local copies, waits for them, and re-layouts  41.8 us (8%)
  other arithmetic  32.5 us (6%)
  between operations  21.3 us (4%)
    dot_general x36, matrix products, product(): jnp.einsum(formula, operand, matrix, preferred_element_type=jnp.float32)  110 us
    all_to_all x2, waiting for transfers between devices, gradient_set(): lax.all_to_all(z_imag, 'fft', split_axis=2, concat_axis=1, tiled=True)  71 us
    all_to_all x2, waiting for transfers between devices, gradient_set(): lax.all_to_all(z_real, 'fft', split_axis=2, concat_axis=1, tiled=True)  68.7 us
    psum x1, blocking collectives, body(): variance, mean_grad = lax.psum((var_part, grad_part), 'fft')  40.9 us
    all_to_all x2, waiting for transfers between devices, tendency(): lax.all_to_all(y_imag, 'fft', split_axis=0, concat_axis=1, tiled=True)  37.1 us
    pmax x1, blocking collectives, body(): peak_value = lax.pmax(peak_part, 'fft')  30.1 us
    all_to_all x2, starting transfers between devices, gradient_set(): lax.all_to_all(z_imag, 'fft', split_axis=2, concat_axis=1, tiled=True)  22.5 us
    all_to_all x2, waiting for transfers between devices, tendency(): lax.all_to_all(y_real, 'fft', split_axis=0, concat_axis=1, tiled=True)  18.7 us
  transfers between devices with their start and end apart: 9, of which 8 were waited for; matrix products, arithmetic and copies ran while one was open for 14% of the time, Pallas kernels for 0%

commit v1 on v0

v1 whole, which is shorter than its diff:
```python
import functools
import math

import jax
import jax.numpy as jnp
from jax import lax
from jax.experimental import pallas as pl
from jax.experimental.pallas import tpu as pltpu
from jax.sharding import PartitionSpec as P

MESH = pl.DeviceIdType.MESH
cfl_number = 0.2


def twiddle(size_in, size_out, length):
    row_index = jnp.arange(size_in, dtype=jnp.int32)[:, None]
    col_index = jnp.arange(size_out, dtype=jnp.int32)[None, :]
    angles = (row_index * col_index % length).astype(jnp.float32) * (2.0 * math.pi / length)
    norming = 1.0 / math.sqrt(length)
    return (jnp.cos(angles) * norming, jnp.sin(angles) * norming)


def build_tables(length):
    half_len = length // 2
    full_cos, full_sin = twiddle(length, length, length)
    inv_cos, inv_sin = twiddle(half_len, length, length)
    weight = jnp.where(jnp.arange(half_len, dtype=jnp.int32) == 0, 1.0, 2.0).astype(jnp.float32)[
        :, None
    ]
    fwd_cos, fwd_sin = twiddle(length, half_len, length)
    listed = (full_cos, full_sin, inv_cos * weight, inv_sin * weight, fwd_cos, fwd_sin)
    return tuple((matrix.astype(jnp.bfloat16) for matrix in listed))


def dot(a, b):
    return jnp.dot(a, b, preferred_element_type=jnp.float32)


def stage_kernel(n, m, rows, chunk, band, first, *refs):
    if first:
        (send, vel, stat_in, inv_y, inv_x, fwd_x, fwd_y,
         gout, uall, stat_out,
         recv, fsend, peak, stat, s_send, s_recv, f_send, f_recv, l_sem, u_send, u_recv, u_loc,
         t_send, t_recv, t_loc) = refs
    else:
        (send, uall, inv_y, inv_x, fwd_x, fwd_y,
         gout,
         recv, fsend, s_send, s_recv, f_send, f_recv, l_sem) = refs
    length = n * rows
    half = length // 2
    count = rows // chunk
    me = lax.axis_index("fft")
    mine = lax.axis_index("scal")

    def inside(d):
        return jnp.logical_or(d * rows <= band, (d + 1) * rows - 1 >= length - band)

    barrier = pltpu.get_barrier_semaphore()

    def greet(j, carry):
        pl.semaphore_signal(barrier, inc=1, device_id={"fft": lax.rem(me + j, n)}, device_id_type=MESH)
        return carry

    lax.fori_loop(1, n, greet, 0)
    if first:
        def greet_other(j, carry):
            pl.semaphore_signal(
                barrier, inc=1, device_id={"scal": lax.rem(mine + j, m)}, device_id_type=MESH
            )
            return carry

        lax.fori_loop(1, m, greet_other, 0)
        pl.semaphore_wait(barrier, n + m - 2)
    else:
        pl.semaphore_wait(barrier, n - 1)

    def inverse_copy(c, d, slot):
        return pltpu.make_async_remote_copy(
            src_ref=send.at[d, pl.ds(c * chunk, chunk)],
            dst_ref=recv.at[pl.ds(c * chunk, chunk), :, slot],
            send_sem=s_send.at[c, d],
            recv_sem=s_recv.at[c, slot],
            device_id={"fft": d},
            device_id_type=MESH,
        )

    def own_copy(c):
        return pltpu.make_async_copy(
            send.at[me, pl.ds(c * chunk, chunk)], recv.at[pl.ds(c * chunk, chunk), :, me], l_sem.at[0, c]
        )

    def speed_copy(c, s, slot):
        return pltpu.make_async_remote_copy(
            src_ref=vel.at[:, pl.ds(c * chunk, chunk)],
            dst_ref=uall.at[:, pl.ds(c * chunk, chunk), slot],
            send_sem=u_send.at[c, s],
            recv_sem=u_recv.at[c, slot],
            device_id={"scal": s},
            device_id_type=MESH,
        )

    def own_speed(c):
        return pltpu.make_async_copy(
            vel.at[:, pl.ds(c * chunk, chunk)], uall.at[:, pl.ds(c * chunk, chunk), mine], u_loc.at[c]
        )

    def forward_copy(c, d, slot):
        return pltpu.make_async_remote_copy(
            src_ref=fsend.at[d, pl.ds(c * chunk, chunk)],
            dst_ref=gout.at[slot, pl.ds(c * chunk, chunk)],
            send_sem=f_send.at[c, d],
            recv_sem=f_recv.at[c, slot],
            device_id={"fft": d},
            device_id_type=MESH,
        )

    def own_forward(c):
        return pltpu.make_async_copy(
            fsend.at[me, pl.ds(c * chunk, chunk)], gout.at[me, pl.ds(c * chunk, chunk)], l_sem.at[1, c]
        )

    def stat_copy(d, slot):
        return pltpu.make_async_remote_copy(
            src_ref=stat,
            dst_ref=stat_out.at[slot],
            send_sem=t_send.at[d],
            recv_sem=t_recv.at[slot],
            device_id={"fft": d},
            device_id_type=MESH,
        )

    def start_chunk(c, carry):
        def one(j, inner):
            inverse_copy(c, lax.rem(me + j, n), me).start()
            return inner

        lax.fori_loop(1, n, one, 0)
        own_copy(c).start()
        if first:
            def two(j, inner):
                speed_copy(c, lax.rem(mine + j, m), mine).start()
                return inner

            lax.fori_loop(1, m, two, 0)
            own_speed(c).start()
        return carry

    lax.fori_loop(0, count, start_chunk, 0)

    if first:
        peak[...] = jnp.zeros_like(peak)

    @pl.when(jnp.logical_not(inside(me)))
    def _():
        gout[...] = jnp.zeros_like(gout)

    row = lax.broadcasted_iota(jnp.int32, (length, half), 0)
    ky = jnp.where(row < half, row, row - length).astype(jnp.float32)
    kx = lax.broadcasted_iota(jnp.int32, (length, half), 1).astype(jnp.float32)

    def pair(z):
        parts = []
        for p in range(2):
            block = recv[z + p].reshape(2 * length, 2 * half)
            w_real = block[:length, :half].astype(jnp.float32)
            w_imag = block[length:, :half].astype(jnp.float32)
            turned = jnp.concatenate(
                [(-ky * w_imag).astype(jnp.bfloat16), (ky * w_real).astype(jnp.bfloat16)], axis=0
            )
            parts += [block, turned]
        section = dot(inv_y[...], jnp.concatenate(parts, axis=1))
        halves = []
        for p in range(2):
            at = 3 * half * p
            w_real = section[:length, at : at + half]
            w_imag = section[length:, at : at + half]
            sides = [
                (-kx * w_imag, kx * w_real),
                (section[:length, at + 2 * half : at + 3 * half], section[length:, at + 2 * half : at + 3 * half]),
                (section[:length, at + half : at + 2 * half], section[length:, at + half : at + 2 * half]),
            ]
            total = None
            square = None
            for i, (re, im) in enumerate(sides):
                lhs = jnp.concatenate([re.astype(jnp.bfloat16), im.astype(jnp.bfloat16)], axis=1)
                grad = dot(lhs, inv_x[...])
                u = uall[i, z + p].reshape(length, length).astype(jnp.float32)
                total = u * grad if total is None else total + u * grad
                if first:
                    square = grad * grad if square is None else square + grad * grad
            if first:
                peak[...] = jnp.maximum(peak[...], jnp.max(square.reshape(length // 8, 8, length), axis=0))
            flat = dot(total.astype(jnp.bfloat16), fwd_x[...]).astype(jnp.bfloat16)
            halves.append(jnp.concatenate([flat[:, :half], flat[:, half:]], axis=0))
        out = dot(fwd_y[...], jnp.concatenate(halves, axis=1)).astype(jnp.bfloat16)
        for p in range(2):
            for q in range(2):
                fsend[:, z + p, q] = out[q * length : (q + 1) * length, p * half : (p + 1) * half].reshape(
                    n, rows, half
                )

    def run_chunk(c, carry):
        def arrive(j, inner):
            inverse_copy(c, lax.rem(me + j, n), lax.rem(me + n - j, n)).wait_recv()
            return inner

        lax.fori_loop(1, n, arrive, 0)
        own_copy(c).wait()
        if first:
            def arrive_speed(j, inner):
                speed_copy(c, lax.rem(mine + j, m), lax.rem(mine + m - j, m)).wait_recv()
                return inner

            lax.fori_loop(1, m, arrive_speed, 0)
            own_speed(c).wait()

        def one(i, inner):
            pair(c * chunk + 2 * i)
            return inner

        lax.fori_loop(0, chunk // 2, one, 0)

        def leave(j, inner):
            d = lax.rem(me + j, n)

            @pl.when(inside(d))
            def _():
                forward_copy(c, d, me).start()

            return inner

        lax.fori_loop(1, n, leave, 0)

        @pl.when(inside(me))
        def _():
            own_forward(c).start()

        return carry

    lax.fori_loop(0, count, run_chunk, 0)

    if first:
        line = lax.broadcasted_iota(jnp.int32, stat.shape, 0)
        largest = jnp.sqrt(jnp.max(peak[...], keepdims=True))
        stat[...] = jnp.where(line == 2, largest, stat_in[...])

        def tell(j, carry):
            stat_copy(lax.rem(me + j, n), me).start()
            return carry

        lax.fori_loop(1, n, tell, 0)
        pltpu.make_async_copy(stat, stat_out.at[me], t_loc).start()

    def finish(c, carry):
        def one(j, inner):
            d = lax.rem(me + j, n)
            inverse_copy(c, d, me).wait_send()

            @pl.when(inside(d))
            def _():
                forward_copy(c, d, me).wait_send()

            @pl.when(inside(me))
            def _():
                forward_copy(c, d, lax.rem(me + n - j, n)).wait_recv()

            return inner

        lax.fori_loop(1, n, one, 0)

        @pl.when(inside(me))
        def _():
            own_forward(c).wait()

        if first:
            def two(j, inner):
                speed_copy(c, lax.rem(mine + j, m), mine).wait_send()
                return inner

            lax.fori_loop(1, m, two, 0)
        return carry

    lax.fori_loop(0, count, finish, 0)

    if first:
        def told(j, carry):
            stat_copy(lax.rem(me + j, n), me).wait_send()
            stat_copy(lax.rem(me + j, n), lax.rem(me + n - j, n)).wait_recv()
            return carry

        lax.fori_loop(1, n, told, 0)
        pltpu.make_async_copy(stat, stat_out.at[me], t_loc).wait()


def run_stage(n, m, rows, first, send, speeds, tables, stat_in=None):
    length = n * rows
    half = length // 2
    chunk = max(2, rows // 4)
    count = rows // chunk
    band = length // 3
    vmem = pl.BlockSpec(memory_space=pltpu.VMEM)
    hbm = pl.BlockSpec(memory_space=pl.ANY)
    dma = pltpu.SemaphoreType.DMA
    out_shape = [jax.ShapeDtypeStruct((n, rows, 2, rows, half), jnp.bfloat16)]
    scratch = [
        pltpu.VMEM((rows, 2, n, rows, 2 * half), jnp.bfloat16),
        pltpu.VMEM((n, rows, 2, rows, half), jnp.bfloat16),
    ]
    sems = [dma((count, n)), dma((count, n)), dma((count, n)), dma((count, n)), dma((2, count))]
    if first:
        operands = (send, speeds, stat_in) + tables
        in_specs = [hbm, hbm, vmem] + [vmem] * 4
        out_shape += [
            jax.ShapeDtypeStruct((3, rows, m, length // m, length), jnp.bfloat16),
            jax.ShapeDtypeStruct((n, 8, 128), jnp.float32),
        ]
        scratch += [pltpu.VMEM((8, length), jnp.float32), pltpu.VMEM((8, 128), jnp.float32)]
        sems += [dma((count, m)), dma((count, m)), dma((count,)), dma((n,)), dma((n,)), dma]
    else:
        operands = (send, speeds) + tables
        in_specs = [hbm, vmem] + [vmem] * 4
    return pl.pallas_call(
        functools.partial(stage_kernel, n, m, rows, chunk, band, first),
        out_shape=out_shape,
        in_specs=in_specs,
        out_specs=[vmem] * len(out_shape),
        scratch_shapes=scratch + sems,
        compiler_params=pltpu.CompilerParams(
            collective_id=0 if first else 1,
            has_side_effects=True,
            vmem_limit_bytes=56 * 1024 * 1024,
        ),
        name="stage_one" if first else "stage_two",
    )(*operands)


def body(n, m, scalar_state, velocity, species, kappa_table, dealias_bound):
    rows = scalar_state.shape[2]
    length = scalar_state.shape[3]
    half = length // 2
    total_count = kappa_table.shape[0]
    full_cos, full_sin, inv_cos, inv_sin, fwd_cos, fwd_sin = build_tables(length)
    inv_y = jnp.concatenate(
        [jnp.concatenate([full_cos, -full_sin], axis=1), jnp.concatenate([full_sin, full_cos], axis=1)], axis=0
    )
    fwd_y = inv_y.T
    inv_x = jnp.concatenate([inv_cos, -inv_sin], axis=0)
    fwd_x = jnp.concatenate([fwd_cos, -fwd_sin], axis=1)
    inv_z = inv_y.reshape(2, length, 2 * length).transpose(1, 0, 2).reshape(2 * length, 2 * length)
    fwd_z = fwd_y.reshape(2 * length, 2, length).transpose(0, 2, 1).reshape(2, length, 2 * length)
    tables = (inv_y, inv_x, fwd_x, fwd_y)
    ky_index = lax.axis_index("fft") * rows + jnp.arange(rows, dtype=jnp.int32)
    ky_wave = jnp.where(ky_index < half, ky_index, ky_index - length).astype(jnp.float32)[:, None, None]
    kz_index = jnp.arange(length, dtype=jnp.int32)
    kz_wave = jnp.where(kz_index < half, kz_index, kz_index - length).astype(jnp.float32)[None, :, None]
    kx_wave = jnp.arange(half, dtype=jnp.int32).astype(jnp.float32)[None, None, :]
    ksquare = kx_wave * kx_wave + ky_wave * ky_wave + kz_wave * kz_wave
    weight = jnp.where(kx_wave == 0.0, 1.0, 2.0).astype(jnp.float32)
    cell_count = float(length) ** 3
    step_size = cfl_number * 2.0 * math.pi / length

    def z_inverse(real_part, imag_part):
        plain = jnp.concatenate([real_part, imag_part], axis=1)
        deriv = jnp.concatenate([-kz_wave * imag_part, kz_wave * real_part], axis=1)
        both = jnp.concatenate([plain, deriv], axis=2).astype(jnp.bfloat16)
        result = jnp.einsum("ab,ybx->ayx", inv_z, both, preferred_element_type=jnp.float32)
        return result.astype(jnp.bfloat16).reshape(n, rows, 2, rows, 2 * half)

    def z_forward(pieces, bound):
        result = jnp.einsum(
            "rkb,byx->rykx",
            fwd_z,
            pieces.reshape(2 * length, rows, half),
            preferred_element_type=jnp.float32,
        )
        keep = ksquare <= bound * bound
        return jnp.where(keep, -result[0], 0.0), jnp.where(keep, -result[1], 0.0)

    start_real = scalar_state[0, 0]
    start_imag = scalar_state[0, 1]
    bound = dealias_bound[0].astype(jnp.float32)
    energy = weight * (start_real * start_real + start_imag * start_imag)
    local_var = jnp.sum(energy) / cell_count
    local_grad = jnp.sum(ksquare * energy) / cell_count
    line = jnp.arange(8, dtype=jnp.int32)[:, None]
    stat_in = jnp.broadcast_to(jnp.where(line == 0, local_var, local_grad), (8, 128))
    pieces, speeds, stats = run_stage(
        n, m, rows, True, z_inverse(start_real, start_imag), velocity, tables, stat_in
    )
    variance = jnp.sum(stats[:, 0, 0])
    mean_grad = jnp.sum(stats[:, 1, 0])
    peak_value = jnp.max(stats[:, 2, 0])
    matches = species[0] == jnp.arange(total_count, dtype=jnp.int32)
    base_kappa = jnp.sum(jnp.where(matches, kappa_table, 0.0))
    kappa = base_kappa * peak_value * jnp.sqrt(variance) / (mean_grad + 1e-06)
    factor = jnp.exp(-kappa * ksquare * step_size)
    first_real, first_imag = z_forward(pieces, bound)
    mid_real = factor * (start_real + step_size * first_real)
    mid_imag = factor * (start_imag + step_size * first_imag)
    (again,) = run_stage(n, m, rows, False, z_inverse(mid_real, mid_imag), speeds, tables)
    second_real, second_imag = z_forward(again, bound)
    new_real = factor * start_real + 0.5 * step_size * (factor * first_real + second_real)
    new_imag = factor * start_imag + 0.5 * step_size * (factor * first_imag + second_imag)
    return (jnp.stack([new_real, new_imag])[None], kappa[None])


def solution(mesh):
    placed = (
        P("scal", None, "fft", None, None),
        P(None, "fft", "scal", None),
        P("scal"),
        P(),
        P("scal"),
    )
    return jax.shard_map(
        functools.partial(body, mesh.shape["fft"], mesh.shape["scal"]),
        mesh=mesh,
        in_specs=placed,
        out_specs=(P("scal", None, "fft", None, None), P("scal")),
        check_vma=False,
    )
```

time: 554 us -> 335 us (0.60); the launches traced: 544 us -> 334 us
  Pallas kernels: 0 us -> 273 us
  waiting for transfers between devices: 202 us -> 0 us
  matrix products: 110 us -> 9.02 us
  blocking collectives: 71 us -> 0 us
  starting transfers between devices: 65.7 us -> 0 us
  other arithmetic: 32.5 us -> 17.5 us
  local copies, waits for them, and re-layouts: 41.8 us -> 27.3 us
  between operations: 21.3 us -> 7.2 us
    pallas_call x0 -> x2, Pallas kernels: none -> 273 us  [run_stage(): pl.pallas_call(functools.partial(stage_kernel, n, m, rows, chunk, band, f...]
    all_to_all x8 -> x0, waiting for transfers between devices: 195 us -> none  [the longest x2 71 us: gradient_set(): lax.all_to_all(z_imag, 'fft', split_axis=2, concat_axis=1, tiled=True)]
    dot_general x36 -> x4, matrix products: 110 us -> 9.02 us  [the longest x2 6.45 us: z_inverse(): jnp.einsum('ab,ybx->ayx', inv_z, both, preferred_element_type=jnp.float32)]
    all_to_all x8 -> x0, starting transfers between devices: 65.2 us -> none  [the longest x2 22.5 us: gradient_set(): lax.all_to_all(z_imag, 'fft', split_axis=2, concat_axis=1, tiled=True)]
    psum x1 -> x0, blocking collectives: 40.9 us -> none  [body(): variance, mean_grad = lax.psum((var_part, grad_part), 'fft')]
    pmax x1 -> x0, blocking collectives: 30.1 us -> none  [body(): peak_value = lax.pmax(peak_part, 'fft')]
    all_to_all x8 -> x0, local copies, waits for them, and re-layouts: 12.9 us -> none  [the longest x2 4.81 us: gradient_set(): lax.all_to_all(z_real, 'fft', split_axis=2, concat_axis=1, tiled=True)]
    convert_element_type x12 -> x2, local copies, waits for them, and re-layouts: 18.2 us -> 8.86 us  [z_inverse(): return result.astype(jnp.bfloat16).reshape(n, rows, 2, rows, 2 * half)]
  transfers between devices with their start and end apart: 9 -> 0, of which waited for: 8 -> 0; matrix products, arithmetic and copies ran while one was open for 14% -> 0% of each run, Pallas kernels for 0% -> 0%
where the time goes in v1:
time: 335 us; the launch traced here: 334 us
  Pallas kernels  273 us (81%)
  local copies, waits for them, and re-layouts  27.3 us (8%)
  other arithmetic  17.5 us (5%)
  matrix products  9.02 us (3%)
  between operations  7.2 us (2%)
    pallas_call x2, Pallas kernels, run_stage(): pl.pallas_call(functools.partial(stage_kernel, n, m, rows, chunk, band, f...  273 us
    convert_element_type x2, local copies, waits for them, and re-layouts, z_inverse(): return result.astype(jnp.bfloat16).reshape(n, rows, 2, rows, 2 * half)  8.86 us

profile of v1, /device:TPU:0, one launch (start us, length us, event | category | flops | bytes accessed | tf_op | source)
XLA Modules:
  0.0 334.0 jit_solution(7630162256279417919)
XLA Ops:
  1.9 1.3 fusion.78
  6.2 1.0 fusion.76
  7.2 1.1 multiply_convert_fusion.2
  8.4 1.0 copy.19.refs_3_.refs_2_
  9.5 1.1 copy.17
  11.0 1.1 copy.20
  13.1 2.7 bitcast_convert_fusion.1
  16.6 3.1 fusion.55
  21.0 3.9 %fusion.19 = bf16[512,16,256]{2,0,1:T(8,128)(2,1)S(1)} fusion(bf16[512,512,1]{1,0,2:T(8,128)(2,1)S(1)} %reshape.156, bf16[16,256,128]{2,1,0:T(8,128)(2,1)} %get-tuple-element.21, bf16[16,256,128]{2,1,0:T(8,128)(2,1)} %get-tuple-element.22, bf16[16,256,128]{2,1,0:T(8,128)(2,1)S(1)} %get-tuple-element.24, bf16[16,256,128]{2,1,0:T(8,128)(2,1)S(1)} %get-tuple-element.23), kind=kOutput, calls=%fused_computation.23 | convolution fusion | flops 2166358016 | bytes 8912896 | tf_op jit(solution)/shard_map/ab,ybx->ayx/dot_general | solution.py:366
  24.9 4.4 %copy.18 = bf16[512,16,256]{2,1,0:T(8,128)(2,1)} copy(bf16[512,16,256]{2,0,1:T(8,128)(2,1)S(1)} %fusion.19) | data formatting | bytes 8388608 | tf_op jit(solution)/shard_map/convert_element_type | solution.py:367
  30.0 140.1 %stage_one.1 = (bf16[16,16,2,16,128]{4,3,2,1,0:T(8,128)(2,1)}, bf16[3,16,2,128,256]{4,3,2,1,0:T(8,128)(2,1)}, f32[16,8,128]{2,1,0:T(8,128)}) custom-call(bf16[16,16,2,16,256]{4,3,2,1,0:T(8,128)(2,1)} %bitcast.75, bf16[3,16,128,256]{3,2,1,0:T(8,128)(2,1)} %refs_1_.1, f32[8,128]{1,0:T(8,128)} %broadcast_in_dim.60.refs_2_, ...), custom_call_target="tpu_custom_call" | custom-call | tf_op jit(solution)/shard_map/stage_one/pallas_call | solution.py:322
  170.1 1.6 slice_reduce_fusion
  174.3 3.0 copy.21
  177.4 1.3 convolution_bitcast_fusion.1
  178.6 0.9 copy-done.3
  179.5 1.5 fusion.89
  182.2 2.6 fusion.16
  184.8 4.4 %copy.24 = bf16[512,16,256]{2,1,0:T(8,128)(2,1)} copy(bf16[512,16,256]{2,0,1:T(8,128)(2,1)S(1)} %fusion.16) | data formatting | bytes 8388608 | tf_op jit(solution)/shard_map/convert_element_type | solution.py:367
  189.2 132.9 %stage_two.1 = bf16[16,16,2,16,128]{4,3,2,1,0:T(8,128)(2,1)} custom-call(bf16[16,16,2,16,256]{4,3,2,1,0:T(8,128)(2,1)} %bitcast.74, bf16[3,16,2,128,256]{4,3,2,1,0:T(8,128)(2,1)} %get-tuple-element.7.refs_1_, bf16[512,512]{1,0:T(8,128)(2,1)} %copy.19.refs_3_.refs_2_, bf16[256,256]{1,0:T(8,128)(2,1)} %get-tuple-element.31.refs_4_.refs_3_, ...), custom_call_target="tpu_custom_call" | custom-call | tf_op jit(solution)/shard_map/stage_two/pallas_call | solution.py:322
  322.1 3.0 copy.26
  325.1 1.3 convolution_bitcast_fusion
  327.3 1.3 copy-done.4
  328.6 2.0 fusion.37
  330.6 2.3 maximum_bitcast_fusion
  (32 shorter events, 7.9 us)
Async XLA Ops:
  8.3 2.5 copy-start.5
  13.1 3.5 %copy-start.2 = (f32[1,2,16,256,128]{4,3,2,1,0:T(8,128)S(1)}, f32[1,2,16,256,128]{4,3,2,1,0:T(8,128)}, u32[]{:S(2)}) copy-start(f32[1,2,16,256,128]{4,3,2,1,0:T(8,128)} %param.5) | copy-start | bytes 12582916
  177.3 2.2 copy-start.3
  179.5 2.0 copy-start
  325.1 2.2 copy-start.1
  325.1 3.5 %copy-start.4 = (f32[1,2,16,256,128]{4,3,2,1,0:T(8,128)S(1)}, f32[1,2,16,256,128]{4,3,2,1,0:T(8,128)}, u32[]{:S(2)}) copy-start(f32[1,2,16,256,128]{4,3,2,1,0:T(8,128)} %param.5) | copy-start | bytes 12582916

commit v2 on v1

--- a/solution.py
+++ b/solution.py
@@ -1,5 +1,7 @@
 import functools
 import math
+
+import numpy as np
 
 import jax
 import jax.numpy as jnp
@@ -13,23 +15,27 @@
 
 
 def twiddle(size_in, size_out, length):
-    row_index = jnp.arange(size_in, dtype=jnp.int32)[:, None]
-    col_index = jnp.arange(size_out, dtype=jnp.int32)[None, :]
-    angles = (row_index * col_index % length).astype(jnp.float32) * (2.0 * math.pi / length)
-    norming = 1.0 / math.sqrt(length)
-    return (jnp.cos(angles) * norming, jnp.sin(angles) * norming)
+    row_index = np.arange(size_in, dtype=np.int32)[:, None]
+    col_index = np.arange(size_out, dtype=np.int32)[None, :]
+    angles = (row_index * col_index % length).astype(np.float32) * np.float32(2.0 * math.pi / length)
+    norming = np.float32(1.0 / math.sqrt(length))
+    return (np.cos(angles) * norming, np.sin(angles) * norming)
 
 
 def build_tables(length):
-    half_len = length // 2
+    half = length // 2
+    quarter = half // 4
     full_cos, full_sin = twiddle(length, length, length)
-    inv_cos, inv_sin = twiddle(half_len, length, length)
-    weight = jnp.where(jnp.arange(half_len, dtype=jnp.int32) == 0, 1.0, 2.0).astype(jnp.float32)[
-        :, None
+    inv_cos, inv_sin = twiddle(half, length, length)
+    weight = np.where(np.arange(half) == 0, 1.0, 2.0).astype(np.float32)[:, None]
+    fwd_cos, fwd_sin = twiddle(length, half, length)
+    inv_y = np.block([[full_cos, -full_sin], [full_sin, full_cos]])
+    inv_x = np.concatenate([inv_cos * weight, -inv_sin * weight], axis=0)
+    orders = [
+        np.concatenate([((p - l - 1) % 4) * quarter + np.arange(quarter) for l in range(4)]) for p in range(4)
     ]
-    fwd_cos, fwd_sin = twiddle(length, half_len, length)
-    listed = (full_cos, full_sin, inv_cos * weight, inv_sin * weight, fwd_cos, fwd_sin)
-    return tuple((matrix.astype(jnp.bfloat16) for matrix in listed))
+    fwd_x = np.stack([np.concatenate([fwd_cos[:, o], -fwd_sin[:, o]], axis=1) for o in orders])
+    return tuple(jnp.asarray(t.astype(np.float32).astype(jnp.bfloat16)) for t in (inv_y, inv_x, fwd_x))
 
 
 def dot(a, b):
@@ -40,20 +46,35 @@
     if first:
         (send, vel, stat_in, inv_y, inv_x, fwd_x, fwd_y,
          gout, uall, stat_out,
-         recv, fsend, peak, stat, s_send, s_recv, f_send, f_recv, l_sem, u_send, u_recv, u_loc,
+         recv, fsend, raw, packed, peak, stat, s_send, s_recv, f_send, f_recv, l_sem, u_send, u_recv, u_loc,
          t_send, t_recv, t_loc) = refs
     else:
         (send, uall, inv_y, inv_x, fwd_x, fwd_y,
          gout,
-         recv, fsend, s_send, s_recv, f_send, f_recv, l_sem) = refs
+         recv, fsend, raw, packed, s_send, s_recv, f_send, f_recv, l_sem) = refs
     length = n * rows
     half = length // 2
     count = rows // chunk
     me = lax.axis_index("fft")
     mine = lax.axis_index("scal")
 
-    def inside(d):
-        return jnp.logical_or(d * rows <= band, (d + 1) * rows - 1 >= length - band)
+    groups = rows // 4
+    quarter = half // 4
+
+    def needed(d, t):
+        low = d * rows
+        least = jnp.where(low < half, low, length - low - rows + 1)
+        return (t * quarter) ** 2 + least * least <= band * band
+
+    def by_tiles(d, act):
+        for k in range(1, 4):
+            wanted = needed(d, k - 1)
+            if k < 3:
+                wanted = jnp.logical_and(wanted, jnp.logical_not(needed(d, k)))
+
+            @pl.when(wanted)
+            def _():
+                act(k)
 
     barrier = pltpu.get_barrier_semaphore()
 
@@ -76,8 +97,8 @@
 
     def inverse_copy(c, d, slot):
         return pltpu.make_async_remote_copy(
-            src_ref=send.at[d, pl.ds(c * chunk, chunk)],
-            dst_ref=recv.at[pl.ds(c * chunk, chunk), :, slot],
+            src_ref=send.at[:, d, pl.ds(c * chunk, chunk)],
+            dst_ref=recv.at[:, pl.ds(c * chunk, chunk), slot],
             send_sem=s_send.at[c, d],
             recv_sem=s_recv.at[c, slot],
             device_id={"fft": d},
@@ -86,7 +107,7 @@
 
     def own_copy(c):
         return pltpu.make_async_copy(
-            send.at[me, pl.ds(c * chunk, chunk)], recv.at[pl.ds(c * chunk, chunk), :, me], l_sem.at[0, c]
+            send.at[:, me, pl.ds(c * chunk, chunk)], recv.at[:, pl.ds(c * chunk, chunk), me], l_sem.at[0, c]
         )
 
     def speed_copy(c, s, slot):
@@ -104,20 +125,18 @@
             vel.at[:, pl.ds(c * chunk, chunk)], uall.at[:, pl.ds(c * chunk, chunk), mine], u_loc.at[c]
         )
 
-    def forward_copy(c, d, slot):
+    def forward_copy(g, d, slot, k):
         return pltpu.make_async_remote_copy(
-            src_ref=fsend.at[d, pl.ds(c * chunk, chunk)],
-            dst_ref=gout.at[slot, pl.ds(c * chunk, chunk)],
-            send_sem=f_send.at[c, d],
-            recv_sem=f_recv.at[c, slot],
+            src_ref=fsend.at[d, g, pl.ds(0, k)],
+            dst_ref=raw.at[slot, g, pl.ds(0, k)],
+            send_sem=f_send.at[g, d],
+            recv_sem=f_recv.at[g, slot],
             device_id={"fft": d},
             device_id_type=MESH,
         )
 
-    def own_forward(c):
-        return pltpu.make_async_copy(
-            fsend.at[me, pl.ds(c * chunk, chunk)], gout.at[me, pl.ds(c * chunk, chunk)], l_sem.at[1, c]
-        )
+    def own_forward(g):
+        return pltpu.make_async_copy(fsend.at[me, g], raw.at[me, g], l_sem.at[1, g])
 
     def stat_copy(d, slot):
         return pltpu.make_async_remote_copy(
@@ -150,18 +169,31 @@
     if first:
         peak[...] = jnp.zeros_like(peak)
 
-    @pl.when(jnp.logical_not(inside(me)))
-    def _():
-        gout[...] = jnp.zeros_like(gout)
+    for t in range(3):
+        @pl.when(jnp.logical_not(needed(me, t)))
+        def _():
+            def clear(j, carry):
+                raw[lax.rem(me + j, n), :, t] = jnp.zeros((groups, 2, rows, half), jnp.bfloat16)
+                return carry
+
+            lax.fori_loop(1, n, clear, 0)
 
     row = lax.broadcasted_iota(jnp.int32, (length, half), 0)
     ky = jnp.where(row < half, row, row - length).astype(jnp.float32)
     kx = lax.broadcasted_iota(jnp.int32, (length, half), 1).astype(jnp.float32)
 
-    def pair(z):
+    lane = lax.broadcasted_iota(jnp.int32, (2 * length, half), 1) // quarter
+
+    def pick(choices):
+        result = choices[-1]
+        for i in range(len(choices) - 2, -1, -1):
+            result = jnp.where(lane == i, choices[i], result)
+        return result
+
+    def pair(z, h):
         parts = []
         for p in range(2):
-            block = recv[z + p].reshape(2 * length, 2 * half)
+            block = jnp.concatenate([recv[q, z + p].reshape(length, 2 * half) for q in range(2)], axis=0)
             w_real = block[:length, :half].astype(jnp.float32)
             w_imag = block[length:, :half].astype(jnp.float32)
             turned = jnp.concatenate(
@@ -190,54 +222,49 @@
                     square = grad * grad if square is None else square + grad * grad
             if first:
                 peak[...] = jnp.maximum(peak[...], jnp.max(square.reshape(length // 8, 8, length), axis=0))
-            flat = dot(total.astype(jnp.bfloat16), fwd_x[...]).astype(jnp.bfloat16)
+            flat = dot(total.astype(jnp.bfloat16), fwd_x[2 * h + p]).astype(jnp.bfloat16)
             halves.append(jnp.concatenate([flat[:, :half], flat[:, half:]], axis=0))
-        out = dot(fwd_y[...], jnp.concatenate(halves, axis=1)).astype(jnp.bfloat16)
-        for p in range(2):
+        packed[h] = dot(fwd_y[...], jnp.concatenate(halves, axis=1))
+
+    def run_group(g, carry):
+        def one_pair(h, outer):
+            c = 2 * g + h
+
+            def arrive(j, inner):
+                inverse_copy(c, lax.rem(me + j, n), lax.rem(me + n - j, n)).wait_recv()
+                return inner
+
+            lax.fori_loop(1, n, arrive, 0)
+            own_copy(c).wait()
+            if first:
+                def arrive_speed(j, inner):
+                    speed_copy(c, lax.rem(mine + j, m), lax.rem(mine + m - j, m)).wait_recv()
+                    return inner
+
+                lax.fori_loop(1, m, arrive_speed, 0)
+                own_speed(c).wait()
+            pair(c * chunk, h)
+            return outer
+
+        lax.fori_loop(0, 2, one_pair, 0)
+
+        for t in range(3):
+            chosen = [(i + 1 + t) % 4 for i in range(4)]
+            tile = pick([packed[p // 2, :, (p % 2) * half : (p % 2 + 1) * half] for p in chosen])
+            tile = tile.astype(jnp.bfloat16)
             for q in range(2):
-                fsend[:, z + p, q] = out[q * length : (q + 1) * length, p * half : (p + 1) * half].reshape(
-                    n, rows, half
-                )
-
-    def run_chunk(c, carry):
-        def arrive(j, inner):
-            inverse_copy(c, lax.rem(me + j, n), lax.rem(me + n - j, n)).wait_recv()
-            return inner
-
-        lax.fori_loop(1, n, arrive, 0)
-        own_copy(c).wait()
-        if first:
-            def arrive_speed(j, inner):
-                speed_copy(c, lax.rem(mine + j, m), lax.rem(mine + m - j, m)).wait_recv()
-                return inner
-
-            lax.fori_loop(1, m, arrive_speed, 0)
-            own_speed(c).wait()
-
-        def one(i, inner):
-            pair(c * chunk + 2 * i)
-            return inner
-
-        lax.fori_loop(0, chunk // 2, one, 0)
+                fsend[:, g, t, q] = tile[q * length : (q + 1) * length].reshape(n, rows, half)
 
         def leave(j, inner):
             d = lax.rem(me + j, n)
-
-            @pl.when(inside(d))
-            def _():
-                forward_copy(c, d, me).start()
-
+            by_tiles(d, lambda k: forward_copy(g, d, me, k).start())
             return inner
 
         lax.fori_loop(1, n, leave, 0)
-
-        @pl.when(inside(me))
-        def _():
-            own_forward(c).start()
-
-        return carry
-
-    lax.fori_loop(0, count, run_chunk, 0)
+        own_forward(g).start()
+        return carry
+
+    lax.fori_loop(0, groups, run_group, 0)
 
     if first:
         line = lax.broadcasted_iota(jnp.int32, stat.shape, 0)
@@ -251,27 +278,33 @@
         lax.fori_loop(1, n, tell, 0)
         pltpu.make_async_copy(stat, stat_out.at[me], t_loc).start()
 
+    def unpack(g, carry):
+        def one(j, inner):
+            d = lax.rem(me + j, n)
+            by_tiles(me, lambda k: forward_copy(g, d, lax.rem(me + n - j, n), k).wait_recv())
+            return inner
+
+        lax.fori_loop(1, n, one, 0)
+        own_forward(g).wait()
+        tiles = [raw[:, g, t].reshape(2 * length, half).astype(jnp.float32) for t in range(3)]
+        for p in range(4):
+            moved = [
+                pltpu.roll(tiles[t], (2 * t + 1 - p) % 4 * quarter, 1) if (2 * t + 1 - p) % 4 else tiles[t]
+                for t in range(3)
+            ]
+            plane = pick(moved + [jnp.zeros_like(tiles[0])]).astype(jnp.bfloat16).reshape(n, 2, rows, half)
+            for q in range(2):
+                gout[q, :, 4 * g + p] = plane[:, q]
+        return carry
+
+    lax.fori_loop(0, groups, unpack, 0)
+
     def finish(c, carry):
         def one(j, inner):
-            d = lax.rem(me + j, n)
-            inverse_copy(c, d, me).wait_send()
-
-            @pl.when(inside(d))
-            def _():
-                forward_copy(c, d, me).wait_send()
-
-            @pl.when(inside(me))
-            def _():
-                forward_copy(c, d, lax.rem(me + n - j, n)).wait_recv()
-
+            inverse_copy(c, lax.rem(me + j, n), me).wait_send()
             return inner
 
         lax.fori_loop(1, n, one, 0)
-
-        @pl.when(inside(me))
-        def _():
-            own_forward(c).wait()
-
         if first:
             def two(j, inner):
                 speed_copy(c, lax.rem(mine + j, m), mine).wait_send()
@@ -282,6 +315,17 @@
 
     lax.fori_loop(0, count, finish, 0)
 
+    def finish_forward(g, carry):
+        def one(j, inner):
+            d = lax.rem(me + j, n)
+            by_tiles(d, lambda k: forward_copy(g, d, me, k).wait_send())
+            return inner
+
+        lax.fori_loop(1, n, one, 0)
+        return carry
+
+    lax.fori_loop(0, groups, finish_forward, 0)
+
     if first:
         def told(j, carry):
             stat_copy(lax.rem(me + j, n), me).wait_send()
@@ -295,18 +339,21 @@
 def run_stage(n, m, rows, first, send, speeds, tables, stat_in=None):
     length = n * rows
     half = length // 2
-    chunk = max(2, rows // 4)
+    chunk = 2
     count = rows // chunk
+    groups = rows // 4
     band = length // 3
     vmem = pl.BlockSpec(memory_space=pltpu.VMEM)
     hbm = pl.BlockSpec(memory_space=pl.ANY)
     dma = pltpu.SemaphoreType.DMA
-    out_shape = [jax.ShapeDtypeStruct((n, rows, 2, rows, half), jnp.bfloat16)]
+    out_shape = [jax.ShapeDtypeStruct((2, n, rows, rows, half), jnp.bfloat16)]
     scratch = [
-        pltpu.VMEM((rows, 2, n, rows, 2 * half), jnp.bfloat16),
-        pltpu.VMEM((n, rows, 2, rows, half), jnp.bfloat16),
+        pltpu.VMEM((2, rows, n, rows, 2 * half), jnp.bfloat16),
+        pltpu.VMEM((n, groups, 3, 2, rows, half), jnp.bfloat16),
+        pltpu.VMEM((n, groups, 3, 2, rows, half), jnp.bfloat16),
+        pltpu.VMEM((2, 2 * length, 2 * half), jnp.float32),
     ]
-    sems = [dma((count, n)), dma((count, n)), dma((count, n)), dma((count, n)), dma((2, count))]
+    sems = [dma((count, n)), dma((count, n)), dma((groups, n)), dma((groups, n)), dma((2, count))]
     if first:
         operands = (send, speeds, stat_in) + tables
         in_specs = [hbm, hbm, vmem] + [vmem] * 4
@@ -339,16 +386,17 @@
     length = scalar_state.shape[3]
     half = length // 2
     total_count = kappa_table.shape[0]
-    full_cos, full_sin, inv_cos, inv_sin, fwd_cos, fwd_sin = build_tables(length)
-    inv_y = jnp.concatenate(
-        [jnp.concatenate([full_cos, -full_sin], axis=1), jnp.concatenate([full_sin, full_cos], axis=1)], axis=0
+    tables = build_tables(length)
+    tables = lax.optimization_barrier(tables)
+    inv_y = tables[0]
+    fwd_y = jnp.concatenate(
+        [
+            jnp.concatenate([inv_y[:length, :length], inv_y[length:, :length]], axis=1),
+            jnp.concatenate([inv_y[:length, length:], inv_y[:length, :length]], axis=1),
+        ],
+        axis=0,
     )
-    fwd_y = inv_y.T
-    inv_x = jnp.concatenate([inv_cos, -inv_sin], axis=0)
-    fwd_x = jnp.concatenate([fwd_cos, -fwd_sin], axis=1)
-    inv_z = inv_y.reshape(2, length, 2 * length).transpose(1, 0, 2).reshape(2 * length, 2 * length)
-    fwd_z = fwd_y.reshape(2 * length, 2, length).transpose(0, 2, 1).reshape(2, length, 2 * length)
-    tables = (inv_y, inv_x, fwd_x, fwd_y)
+    tables = tables + (fwd_y,)
     ky_index = lax.axis_index("fft") * rows + jnp.arange(rows, dtype=jnp.int32)
     ky_wave = jnp.where(ky_index < half, ky_index, ky_index - length).astype(jnp.float32)[:, None, None]
     kz_index = jnp.arange(length, dtype=jnp.int32)
@@ -363,13 +411,13 @@
         plain = jnp.concatenate([real_part, imag_part], axis=1)
         deriv = jnp.concatenate([-kz_wave * imag_part, kz_wave * real_part], axis=1)
         both = jnp.concatenate([plain, deriv], axis=2).astype(jnp.bfloat16)
-        result = jnp.einsum("ab,ybx->ayx", inv_z, both, preferred_element_type=jnp.float32)
-        return result.astype(jnp.bfloat16).reshape(n, rows, 2, rows, 2 * half)
+        result = jnp.einsum("ab,ybx->ayx", inv_y, both, preferred_element_type=jnp.float32)
+        return result.astype(jnp.bfloat16).reshape(2, n, rows, rows, 2 * half)
 
     def z_forward(pieces, bound):
         result = jnp.einsum(
             "rkb,byx->rykx",
-            fwd_z,
+            fwd_y.reshape(2, length, 2 * length),
             pieces.reshape(2 * length, rows, half),
             preferred_element_type=jnp.float32,
         )

time: 335 us -> 312 us (0.931)
  Pallas kernels: 273 us -> 257 us
  other arithmetic: 17.5 us -> 13.4 us
    pallas_call x2, Pallas kernels: 273 us -> 257 us  [run_stage(): pl.pallas_call(functools.partial(stage_kernel, n, m, rows, chunk, band, f...]
where the time goes in v2:
time: 312 us; the launch traced here: 311 us
  Pallas kernels  257 us (82%)
  local copies, waits for them, and re-layouts  24.4 us (8%)
  other arithmetic  13.4 us (4%)
  matrix products  9 us (3%)
  between operations  7.13 us (2%)
    pallas_call x2, Pallas kernels, run_stage(): pl.pallas_call(functools.partial(stage_kernel, n, m, rows, chunk, band, f...  257 us
    convert_element_type x2, local copies, waits for them, and re-layouts, z_inverse(): return result.astype(jnp.bfloat16).reshape(2, n, rows, rows, 2 * half)  8.86 us
    dot_general x2, matrix products, z_inverse(): jnp.einsum('ab,ybx->ayx', inv_y, both, preferred_element_type=jnp.float32)  6.43 us

profile of v2, /device:TPU:0, one launch (start us, length us, event | category | flops | bytes accessed | tf_op | source)
XLA Modules:
  0.0 311.3 jit_solution(17160324068683359089)
XLA Ops:
  1.9 1.3 fusion.59
  3.4 1.1 fusion.70
  4.4 0.9 maximum_maximum_fusion.refs_6_.refs_5_
  5.3 2.7 bitcast_convert_fusion.1
  8.0 0.7 copy-done.2
  8.7 3.1 %fusion.57 = (f32[]{:T(128)}, f32[]{:T(128)}, bf16[16,256,128]{2,1,0:T(8,128)(2,1)}, bf16[16,256,128]{2,1,0:T(8,128)(2,1)}) fusion(f32[1,2,16,256,128]{4,3,2,1,0:T(8,128)S(1)} %copy-done.2, f32[128]{0:T(128)S(1)} %compare_select_fusion.2, f32[256]{0:T(256)S(1)} %get-tuple-element.34, f32[16,128]{1,0:T(8,128)S(1)} %broadcast_add_fusion, f32[256]{0:T(256)S(1)} %fusion.58, ...), kind=kLoop, calls=%fused_computation.74 | loop fusion | flops 6291454 | bytes 6303240 | tf_op jit(solution)/shard_map/reduce_sum | solution.py:431
  13.2 3.9 %fusion.19 = bf16[512,16,256]{2,0,1:T(8,128)(2,1)S(1)} fusion(bf16[16,256,128]{2,1,0:T(8,128)(2,1)} %get-tuple-element.27, bf16[16,256,128]{2,1,0:T(8,128)(2,1)} %get-tuple-element.28, bf16[16,256,128]{2,1,0:T(8,128)(2,1)S(1)} %get-tuple-element.30, bf16[16,256,128]{2,1,0:T(8,128)(2,1)S(1)} %get-tuple-element.29, bf16[512,512]{1,0:T(8,128)(2,1)S(1)} %copy-done.7), kind=kOutput, calls=%fused_computation.23 | convolution fusion | flops 2166358016 | bytes 8912896 | tf_op jit(solution)/shard_map/ab,ybx->ayx/dot_general | solution.py:414
  17.1 4.4 %copy.10 = bf16[512,16,256]{2,1,0:T(8,128)(2,1)} copy(bf16[512,16,256]{2,0,1:T(8,128)(2,1)S(1)} %fusion.19) | data formatting | bytes 8388608 | tf_op jit(solution)/shard_map/convert_element_type | solution.py:415
  22.2 129.9 %stage_one.1 = (bf16[2,16,16,16,128]{4,3,2,1,0:T(8,128)(2,1)}, bf16[3,16,2,128,256]{4,3,2,1,0:T(8,128)(2,1)}, f32[16,8,128]{2,1,0:T(8,128)}) custom-call(bf16[2,16,16,16,256]{4,3,2,1,0:T(8,128)(2,1)} %bitcast.73, bf16[3,16,128,256]{3,2,1,0:T(8,128)(2,1)} %refs_1_.1, f32[8,128]{1,0:T(8,128)} %broadcast_in_dim.49.refs_2_, ...), custom_call_target="tpu_custom_call" | custom-call | tf_op jit(solution)/shard_map/stage_one/pallas_call | solution.py:369
  152.1 1.6 slice_reduce_fusion
  156.3 3.1 copy.11
  159.3 1.3 convolution_bitcast_fusion.1
  160.6 0.9 copy-done.3
  161.5 1.5 fusion.68
  164.2 0.7 copy-done.8
  164.9 2.5 fusion.16
  167.5 4.4 %copy.13 = bf16[512,16,256]{2,1,0:T(8,128)(2,1)} copy(bf16[512,16,256]{2,0,1:T(8,128)(2,1)S(1)} %fusion.16) | data formatting | bytes 8388608 | tf_op jit(solution)/shard_map/convert_element_type | solution.py:415
  171.9 127.4 %stage_two.1 = bf16[2,16,16,16,128]{4,3,2,1,0:T(8,128)(2,1)} custom-call(bf16[2,16,16,16,256]{4,3,2,1,0:T(8,128)(2,1)} %bitcast.72, bf16[3,16,2,128,256]{4,3,2,1,0:T(8,128)(2,1)} %get-tuple-element.13.refs_1_, bf16[512,512]{1,0:T(8,128)(2,1)} %constant.43.clone.refs_3_.refs_2_, bf16[256,256]{1,0:T(8,128)(2,1)} %constant.44.clone.refs_4_.refs_3_, ...), custom_call_target="tpu_custom_call" | custom-call | tf_op jit(solution)/shard_map/stage_two/pallas_call | solution.py:369
  299.3 3.1 copy.14
  302.4 1.3 convolution_bitcast_fusion
  303.7 0.9 copy-done.1
  304.6 1.3 copy-done.4
  305.9 2.0 fusion.37
  307.9 2.3 maximum_bitcast_fusion
  (23 shorter events, 1.9 us)
Async XLA Ops:
  5.3 3.4 %copy-start.2 = (f32[1,2,16,256,128]{4,3,2,1,0:T(8,128)S(1)}, f32[1,2,16,256,128]{4,3,2,1,0:T(8,128)}, u32[]{:S(2)}) copy-start(f32[1,2,16,256,128]{4,3,2,1,0:T(8,128)} %param.8) | copy-start | bytes 12582916
  8.7 4.4 %copy-start.7 = (bf16[512,512]{1,0:T(8,128)(2,1)S(1)}, bf16[512,512]{1,0:T(8,128)(2,1)}, u32[]{:S(2)}) copy-start(bf16[512,512]{1,0:T(8,128)(2,1)} %constant.43.clone.refs_3_.refs_2_) | copy-start | bytes 1572868
  156.2 3.1 copy-start.5
  159.3 2.2 copy-start.3
  161.5 2.0 copy-start
  163.9 1.0 copy-start.8
  299.3 3.1 copy-start.6
  302.4 2.2 copy-start.1
  302.4 3.5 %copy-start.4 = (f32[1,2,16,256,128]{4,3,2,1,0:T(8,128)S(1)}, f32[1,2,16,256,128]{4,3,2,1,0:T(8,128)}, u32[]{:S(2)}) copy-start(f32[1,2,16,256,128]{4,3,2,1,0:T(8,128)} %param.8) | copy-start | bytes 12582916

commit v3 on v2

--- a/solution.py
+++ b/solution.py
@@ -226,59 +226,7 @@
             halves.append(jnp.concatenate([flat[:, :half], flat[:, half:]], axis=0))
         packed[h] = dot(fwd_y[...], jnp.concatenate(halves, axis=1))
 
-    def run_group(g, carry):
-        def one_pair(h, outer):
-            c = 2 * g + h
-
-            def arrive(j, inner):
-                inverse_copy(c, lax.rem(me + j, n), lax.rem(me + n - j, n)).wait_recv()
-                return inner
-
-            lax.fori_loop(1, n, arrive, 0)
-            own_copy(c).wait()
-            if first:
-                def arrive_speed(j, inner):
-                    speed_copy(c, lax.rem(mine + j, m), lax.rem(mine + m - j, m)).wait_recv()
-                    return inner
-
-                lax.fori_loop(1, m, arrive_speed, 0)
-                own_speed(c).wait()
-            pair(c * chunk, h)
-            return outer
-
-        lax.fori_loop(0, 2, one_pair, 0)
-
-        for t in range(3):
-            chosen = [(i + 1 + t) % 4 for i in range(4)]
-            tile = pick([packed[p // 2, :, (p % 2) * half : (p % 2 + 1) * half] for p in chosen])
-            tile = tile.astype(jnp.bfloat16)
-            for q in range(2):
-                fsend[:, g, t, q] = tile[q * length : (q + 1) * length].reshape(n, rows, half)
-
-        def leave(j, inner):
-            d = lax.rem(me + j, n)
-            by_tiles(d, lambda k: forward_copy(g, d, me, k).start())
-            return inner
-
-        lax.fori_loop(1, n, leave, 0)
-        own_forward(g).start()
-        return carry
-
-    lax.fori_loop(0, groups, run_group, 0)
-
-    if first:
-        line = lax.broadcasted_iota(jnp.int32, stat.shape, 0)
-        largest = jnp.sqrt(jnp.max(peak[...], keepdims=True))
-        stat[...] = jnp.where(line == 2, largest, stat_in[...])
-
-        def tell(j, carry):
-            stat_copy(lax.rem(me + j, n), me).start()
-            return carry
-
-        lax.fori_loop(1, n, tell, 0)
-        pltpu.make_async_copy(stat, stat_out.at[me], t_loc).start()
-
-    def unpack(g, carry):
+    def unpack(g):
         def one(j, inner):
             d = lax.rem(me + j, n)
             by_tiles(me, lambda k: forward_copy(g, d, lax.rem(me + n - j, n), k).wait_recv())
@@ -295,9 +243,65 @@
             plane = pick(moved + [jnp.zeros_like(tiles[0])]).astype(jnp.bfloat16).reshape(n, 2, rows, half)
             for q in range(2):
                 gout[q, :, 4 * g + p] = plane[:, q]
+
+    def run_group(g, carry):
+        def one_pair(h, outer):
+            c = 2 * g + h
+
+            def arrive(j, inner):
+                inverse_copy(c, lax.rem(me + j, n), lax.rem(me + n - j, n)).wait_recv()
+                return inner
+
+            lax.fori_loop(1, n, arrive, 0)
+            own_copy(c).wait()
+            if first:
+                def arrive_speed(j, inner):
+                    speed_copy(c, lax.rem(mine + j, m), lax.rem(mine + m - j, m)).wait_recv()
+                    return inner
+
+                lax.fori_loop(1, m, arrive_speed, 0)
+                own_speed(c).wait()
+            pair(c * chunk, h)
+            return outer
+
+        lax.fori_loop(0, 2, one_pair, 0)
+
+        for t in range(3):
+            chosen = [(i + 1 + t) % 4 for i in range(4)]
+            tile = pick([packed[p // 2, :, (p % 2) * half : (p % 2 + 1) * half] for p in chosen])
+            tile = tile.astype(jnp.bfloat16)
+            for q in range(2):
+                fsend[:, g, t, q] = tile[q * length : (q + 1) * length].reshape(n, rows, half)
+
+        def leave(j, inner):
+            d = lax.rem(me + j, n)
+            by_tiles(d, lambda k: forward_copy(g, d, me, k).start())
+            return inner
+
+        lax.fori_loop(1, n, leave, 0)
+        own_forward(g).start()
+
+        @pl.when(g >= 1)
+        def _():
+            unpack(g - 1)
+
         return carry
 
-    lax.fori_loop(0, groups, unpack, 0)
+    lax.fori_loop(0, groups, run_group, 0)
+
+    if first:
+        line = lax.broadcasted_iota(jnp.int32, stat.shape, 0)
+        largest = jnp.sqrt(jnp.max(peak[...], keepdims=True))
+        stat[...] = jnp.where(line == 2, largest, stat_in[...])
+
+        def tell(j, carry):
+            stat_copy(lax.rem(me + j, n), me).start()
+            return carry
+
+        lax.fori_loop(1, n, tell, 0)
+        pltpu.make_async_copy(stat, stat_out.at[me], t_loc).start()
+
+    unpack(groups - 1)
 
     def finish(c, carry):
         def one(j, inner):
@@ -422,7 +426,7 @@
             preferred_element_type=jnp.float32,
         )
         keep = ksquare <= bound * bound
-        return jnp.where(keep, -result[0], 0.0), jnp.where(keep, -result[1], 0.0)
+        return jnp.where(keep[None], -result, 0.0)
 
     start_real = scalar_state[0, 0]
     start_imag = scalar_state[0, 1]
@@ -442,14 +446,13 @@
     base_kappa = jnp.sum(jnp.where(matches, kappa_table, 0.0))
     kappa = base_kappa * peak_value * jnp.sqrt(variance) / (mean_grad + 1e-06)
     factor = jnp.exp(-kappa * ksquare * step_size)
-    first_real, first_imag = z_forward(pieces, bound)
-    mid_real = factor * (start_real + step_size * first_real)
-    mid_imag = factor * (start_imag + step_size * first_imag)
-    (again,) = run_stage(n, m, rows, False, z_inverse(mid_real, mid_imag), speeds, tables)
-    second_real, second_imag = z_forward(again, bound)
-    new_real = factor * start_real + 0.5 * step_size * (factor * first_real + second_real)
-    new_imag = factor * start_imag + 0.5 * step_size * (factor * first_imag + second_imag)
-    return (jnp.stack([new_real, new_imag])[None], kappa[None])
+    start = scalar_state[0]
+    first = z_forward(pieces, bound)
+    middle = factor[None] * (start + step_size * first)
+    (again,) = run_stage(n, m, rows, False, z_inverse(middle[0], middle[1]), speeds, tables)
+    second = z_forward(again, bound)
+    updated = factor[None] * start + 0.5 * step_size * (factor[None] * first + second)
+    return (updated[None], kappa[None])
 
 
 def solution(mesh):

time: 312 us -> 323 us (1.035)
  matrix products: 9 us -> 21.1 us
  Pallas kernels: 257 us -> 263 us
  other arithmetic: 13.4 us -> 8.43 us
    dot_general x2, matrix products: 2.57 us -> 14.6 us  [z_forward(): jnp.einsum('rkb,byx->rykx', fwd_y.reshape(2, length, 2 * length), pieces....]
    pallas_call x2, Pallas kernels: 257 us -> 263 us  [run_stage(): pl.pallas_call(functools.partial(stage_kernel, n, m, rows, chunk, band, f...]
    unnamed x18 -> x10, local copies, waits for them, and re-layouts: 5.06 us -> 0.13 us
where the time goes in v3:
time: 323 us
  Pallas kernels  263 us (81%)
  local copies, waits for them, and re-layouts  22.4 us (7%)
  matrix products  21.1 us (7%)
  other arithmetic  8.43 us (3%)
  between operations  7.41 us (2%)
    pallas_call x2, Pallas kernels, run_stage(): pl.pallas_call(functools.partial(stage_kernel, n, m, rows, chunk, band, f...  263 us
    dot_general x2, matrix products, z_forward(): jnp.einsum('rkb,byx->rykx', fwd_y.reshape(2, length, 2 * length), pieces....  14.6 us
    convert_element_type x2, local copies, waits for them, and re-layouts, z_inverse(): return result.astype(jnp.bfloat16).reshape(2, n, rows, rows, 2 * half)  8.89 us
    reshape x2, local copies, waits for them, and re-layouts, z_forward(): pieces.reshape(2 * length, rows, half)  8.85 us

profile of v3, /device:TPU:0, one launch (start us, length us, event | category | flops | bytes accessed | tf_op | source)
XLA Modules:
  0.0 322.8 jit_solution(12382387520299504238)
XLA Ops:
  2.3 1.3 fusion.43
  3.6 0.1 broadcast_add_fusion
  3.7 1.1 fusion.50
  4.8 0.9 maximum_maximum_fusion.refs_6_.refs_5_
  5.6 0.4 add_compare_fusion
  6.0 2.5 bitcast_convert_fusion.1
  8.6 0.0 copy-start.3
  8.6 3.1 fusion.41
  13.0 3.9 %fusion.24 = bf16[512,16,256]{2,0,1:T(8,128)(2,1)S(1)} fusion(bf16[16,256,128]{2,1,0:T(8,128)(2,1)} %get-tuple-element.23, bf16[16,256,128]{2,1,0:T(8,128)(2,1)} %get-tuple-element.24, bf16[16,256,128]{2,1,0:T(8,128)(2,1)S(1)} %get-tuple-element.26, bf16[16,256,128]{2,1,0:T(8,128)(2,1)S(1)} %get-tuple-element.25, bf16[512,512]{1,0:T(8,128)(2,1)S(1)} %copy-done.3), kind=kOutput, calls=%fused_computation.29 | convolution fusion | flops 2166358016 | bytes 8912896 | tf_op jit(solution)/shard_map/ab,ybx->ayx/dot_general | solution.py:418
  16.9 4.4 %copy.10 = bf16[512,16,256]{2,1,0:T(8,128)(2,1)} copy(bf16[512,16,256]{2,0,1:T(8,128)(2,1)S(1)} %fusion.24) | data formatting | bytes 8388608 | tf_op jit(solution)/shard_map/convert_element_type | solution.py:419
  21.4 0.7 broadcast_in_dim.61.refs_2_
  22.0 133.1 %stage_one.1 = (bf16[2,16,16,16,128]{4,3,2,1,0:T(8,128)(2,1)}, bf16[3,16,2,128,256]{4,3,2,1,0:T(8,128)(2,1)}, f32[16,8,128]{2,1,0:T(8,128)}) custom-call(bf16[2,16,16,16,256]{4,3,2,1,0:T(8,128)(2,1)} %bitcast.92, bf16[3,16,128,256]{3,2,1,0:T(8,128)(2,1)} %refs_1_.1, f32[8,128]{1,0:T(8,128)} %broadcast_in_dim.61.refs_2_, ...), custom_call_target="tpu_custom_call" | custom-call | tf_op jit(solution)/shard_map/stage_one/pallas_call | solution.py:373
  155.1 1.6 slice_reduce_fusion
  159.3 4.5 %copy.11 = bf16[512,16,128]{0,2,1:T(8,128)(2,1)} copy(bf16[512,16,128]{2,1,0:T(8,128)(2,1)} %bitcast.96) | data formatting | bytes 4194304 | tf_op jit(solution)/shard_map/reshape | solution.py:425
  163.8 0.4 fusion.29
  164.2 6.5 %fusion.20 = (f32[2,16,256,128]{3,2,1,0:T(8,128)S(1)}, f32[16,128,2,256]{1,3,0,2:T(8,128)}) fusion(f32[1,2,16,256,128]{4,3,2,1,0:T(8,128)} %param.8, f32[16,256,128]{2,1,0:T(8,128)S(1)} %fusion.29, pred[16,256,128]{2,1,0:T(8,128)(4,1)S(1)} %add_compare_fusion, bf16[2,256,512,1]{2,1,3,0:T(8,128)(2,1)S(1)} %bitcast.93, bf16[512,16,128]{0,2,1:T(8,128)(2,1)} %copy.11), kind=kOutput, calls=%fused_computation.24 | convolution fusion | flops 1078984704 | bytes 17825792 | tf_op jit(solution)/shard_map/rkb,byx->rykx/dot_general | solution.py:422
  170.7 0.6 multiply_convert_fusion.1
  171.3 0.3 fusion.37
  171.7 0.1 copy-done.4
  171.8 2.5 fusion.21
  174.3 4.5 %copy.13 = bf16[512,16,256]{2,1,0:T(8,128)(2,1)} copy(bf16[512,16,256]{2,0,1:T(8,128)(2,1)S(1)} %fusion.21) | data formatting | bytes 8388608 | tf_op jit(solution)/shard_map/convert_element_type | solution.py:419
  178.8 130.3 %stage_two.1 = bf16[2,16,16,16,128]{4,3,2,1,0:T(8,128)(2,1)} custom-call(bf16[2,16,16,16,256]{4,3,2,1,0:T(8,128)(2,1)} %bitcast.91, bf16[3,16,2,128,256]{4,3,2,1,0:T(8,128)(2,1)} %get-tuple-element.13.refs_1_, bf16[512,512]{1,0:T(8,128)(2,1)} %constant.44.clone.refs_3_.refs_2_, bf16[256,256]{1,0:T(8,128)(2,1)} %constant.45.clone.refs_4_.refs_3_, ...), custom_call_target="tpu_custom_call" | custom-call | tf_op jit(solution)/shard_map/stage_two/pallas_call | solution.py:373
  309.1 4.4 %copy.14 = bf16[512,16,128]{0,2,1:T(8,128)(2,1)} copy(bf16[512,16,128]{2,1,0:T(8,128)(2,1)} %bitcast.95) | data formatting | bytes 4194304 | tf_op jit(solution)/shard_map/reshape | solution.py:425
  313.5 8.1 %fusion.19 = f32[1,2,16,256,128]{4,3,2,1,0:T(8,128)} fusion(f32[1,2,16,256,128]{4,3,2,1,0:T(8,128)} %param.8, f32[16,128,2,256]{1,3,0,2:T(8,128)} %get-tuple-element.31, bf16[2,256,512,1]{2,1,3,0:T(8,128)(2,1)S(1)} %bitcast.94, bf16[512,16,128]{0,2,1:T(8,128)(2,1)} %copy.14, f32[16,256,128]{2,1,0:T(8,128)S(1)} %fusion.29, ...), kind=kOutput, calls=%fused_computation.20 | convolution fusion | flops 1083179008 | bytes 17825792 | tf_op jit(solution)/shard_map/rkb,byx->rykx/dot_general | solution.py:422
  (14 shorter events, 0.0 us)
Async XLA Ops:
  0.6 8.0 %copy-start = (f32[1,2,16,256,128]{4,3,2,1,0:T(8,128)S(1)}, f32[1,2,16,256,128]{4,3,2,1,0:T(8,128)}, u32[]{:S(2)}) copy-start(f32[1,2,16,256,128]{4,3,2,1,0:T(8,128)} %param.8) | copy-start | bytes 12582916
  8.6 4.5 %copy-start.3 = (bf16[512,512]{1,0:T(8,128)(2,1)S(1)}, bf16[512,512]{1,0:T(8,128)(2,1)}, u32[]{:S(2)}) copy-start(bf16[512,512]{1,0:T(8,128)(2,1)} %constant.44.clone.refs_3_.refs_2_) | copy-start | bytes 1572868
  155.1 9.1 %copy-start.1 = (bf16[512,512]{1,0:T(8,128)(2,1)S(1)}, bf16[512,512]{1,0:T(8,128)(2,1)}, u32[]{:S(2)}) copy-start(bf16[512,512]{1,0:T(8,128)(2,1)} %maximum_maximum_fusion.refs_6_.refs_5_) | copy-start | bytes 1572868
  170.7 1.0 copy-start.4
  309.1 4.4 %copy-start.2 = (bf16[512,512]{1,0:T(8,128)(2,1)S(1)}, bf16[512,512]{1,0:T(8,128)(2,1)}, u32[]{:S(2)}) copy-start(bf16[512,512]{1,0:T(8,128)(2,1)} %maximum_maximum_fusion.refs_6_.refs_5_) | copy-start | bytes 1572868
